TPU v7x, 32 devices: a whole 2x2x4 slice. The times are simulated.
32 devices in a mesh: row: 4 (over y, core), col: 8 (over z, x).
Axes of the slice: x: 2, y: 2, z: 4, core: 2. Of those that a mesh axis runs over, the one named last changes fastest.
Arguments:
- residuals: bfloat16 [16384, 32], P(('row', 'col')), may hold values from -6 to 6
- intersect_blocks: int32 [32, 4], P(('row', 'col')), may hold values from 0 to 3
- local_inverse: bfloat16 [16384, 1024], P(('row', 'col')), may hold values from -0.1875 to 0.1875
- coarse_basis: float32 [32768, 64], P(('row', 'col')), may hold values from -0.1875 to 0.1875
- coarse_slots: int32 [2048], replicated, may hold values from 0 to 2047, each once
- coarse_inverse: float32 [2048, 2048], P('row', 'col'), may hold values from -0.5 to 0.5
Outputs:
- preconditioned: float32 [16384, 32], P(('row', 'col'))
Inputs may be any that keep to these rules, and one draw needn't show every extreme that they name: `intersect_blocks`: each entry names one of the four owned blocks. `coarse_slots`: every coarse index from 0 to 2047 appears exactly once.
All inputs are finite; a program needn't handle non-finite values.
Results may differ from a plain program's by a relative error of at most 0.0003.
Values may be sent and summed in bfloat16 or wider, within the bound.
A program may use at most 64 MiB of HBM per device.

v0:
```python
import jax
import jax.numpy as jnp
from jax import lax
from jax.sharding import PartitionSpec as P

BLK = 128


def extended(cells, sides, width, closed):
    for axis, dim in sides:
        count = lax.axis_size(axis)
        ends = count if closed else count - 1
        head = lax.slice_in_dim(cells, 0, width, axis=dim)
        tail = lax.slice_in_dim(cells, cells.shape[dim] - width, cells.shape[dim], axis=dim)
        cells = jnp.concatenate(
            [
                lax.ppermute(tail, axis, [(i, (i + 1) % count) for i in range(ends)]),
                cells,
                lax.ppermute(head, axis, [((i + 1) % count, i) for i in range(ends)]),
            ],
            axis=dim,
        )
    return cells


def shards(residuals, intersect_blocks, local_inverse, coarse_basis, coarse_slots, coarse_inverse):
    own_rows = residuals.shape[0]
    rhs_count = residuals.shape[1]
    nev_count = coarse_basis.shape[1]
    blocks = residuals.reshape(own_rows // BLK, BLK, rhs_count)
    send_index = intersect_blocks[0]
    outgoing = jnp.take(blocks, send_index, axis=0)
    padded = extended(outgoing[None, None], (("row", 0), ("col", 1)), 1, False)
    incoming = jnp.stack([padded[0, 1, 0], padded[2, 1, 1], padded[1, 0, 2], padded[1, 2, 3]])
    local_vec = jnp.concatenate([residuals, incoming.reshape(-1, rhs_count)], axis=0)
    schwarz = jnp.dot(local_inverse, local_vec, preferred_element_type=jnp.float32)
    partial_sums = jnp.dot(
        coarse_basis.T, local_vec.astype(jnp.float32), precision=lax.Precision.HIGHEST
    )
    column_width = coarse_inverse.shape[1]
    col_offset = lax.axis_index("col") * column_width

    def add_piece(carry, piece):
        shifted = lax.slice_in_dim(coarse_slots, 0, piece.shape[0], axis=0) - col_offset
        inside = (shifted >= 0) & (shifted < column_width)
        target = jnp.where(inside, shifted, column_width)
        return carry.at[target].add(piece, mode="drop")

    column_part = add_piece(
        jnp.zeros((column_width, rhs_count), jnp.float32),
        jax.tree.map(lambda a: lax.all_gather(a, ("row", "col"), axis=0, tiled=True), partial_sums),
    )
    product = jnp.dot(coarse_inverse, column_part, precision=lax.Precision.HIGHEST)
    row_total = lax.psum(product, "col")
    whole_coarse = lax.all_gather(row_total, "row", axis=0, tiled=True)
    my_slots = lax.dynamic_slice_in_dim(
        coarse_slots, lax.axis_index(("row", "col")) * nev_count, nev_count, 0
    )
    own_coarse = jnp.take(whole_coarse, my_slots, axis=0)
    prolonged = jnp.dot(coarse_basis, own_coarse, precision=lax.Precision.HIGHEST)
    returning = prolonged[own_rows:].reshape(-1, BLK, rhs_count)
    padded_back = extended(returning[None, None], (("row", 0), ("col", 1)), 1, False)
    returned = jnp.stack(
        [padded_back[2, 1, 0], padded_back[0, 1, 1], padded_back[1, 2, 2], padded_back[1, 0, 3]]
    )
    matches = (send_index[:, None] == jnp.arange(own_rows // BLK, dtype=jnp.int32)[None, :]).astype(
        jnp.float32
    )
    added = jnp.einsum("db,dkr->bkr", matches, returned, precision=lax.Precision.HIGHEST)
    return schwarz + prolonged[:own_rows] + added.reshape(own_rows, rhs_count)


def solution(mesh):
    placed = (
        P(("row", "col"), None),
        P(("row", "col"), None),
        P(("row", "col"), None),
        P(("row", "col"), None),
        P(),
        P("row", "col"),
    )
    return jax.shard_map(
        shards, mesh=mesh, in_specs=placed, out_specs=P(("row", "col"), None), check_vma=False
    )
```

profile of v0, /device:TPU:0, one launch (start us, length us, event | category | flops | bytes accessed | tf_op | source)
XLA Modules:
  0.0 212.3 jit_solution(17657866889500280651)
XLA Ops:
  6.5 0.0 copy-start
  6.5 0.0 all-reduce.2.cloned.1.call-start
  6.5 0.8 fusion.18
  7.3 0.0 copy-done.7
  7.3 0.8 copy_bitcast_fusion
  8.1 0.0 copy-start.3
  8.1 0.0 copy-start.6
  8.1 0.6 gather_fusion
  8.7 0.0 copy-start.1
  8.7 0.1 bitcast_select_fusion
  8.8 2.4 %collective-permute-start = (bf16[1,1,4,128,32]{3,4,2,1,0:T(8,128)(2,1)S(1)}, bf16[1,1,4,128,32]{3,4,2,1,0:T(8,128)(2,1)S(1)}, u32[]{:S(2)}, u32[]{:S(2)}) collective-permute-start(bf16[1,1,4,128,32]{3,4,2,1,0:T(8,128)(2,1)S(1)} %bitcast_select_fusion), channel_id=1, source_target_pairs={{0,8},{8,16},{16,24},{1,9},{9,17},{17,25},{2,10},{10,18},{18,26},{... | collective-permute-start | bytes 98312 | tf_op jit(solution)/shard_map/ppermute | solution.py:17
  11.2 1.3 collective-permute-start.1
  12.5 0.0 copy-done.3
  12.5 0.0 copy-done.6
  12.5 0.1 compare_and_fusion
  12.6 0.0 collective-permute-done
  12.6 3.8 %collective-permute-done.1 = bf16[1,1,4,128,32]{3,4,2,1,0:T(8,128)(2,1)S(1)} collective-permute-done((bf16[1,1,4,128,32]{3,4,2,1,0:T(8,128)(2,1)S(1)}, bf16[1,1,4,128,32]{3,4,2,1,0:T(8,128)(2,1)S(1)}, u32[]{:S(2)}, u32[]{:S(2)}) %collective-permute-start.1) | collective-permute-done | bytes 32800 | tf_op jit(solution)/shard_map/ppermute | solution.py:19
  16.4 1.3 collective-permute-start.3
  17.7 4.6 %collective-permute-start.2 = (bf16[3,1,4,128,32]{3,4,2,1,0:T(8,128)(2,1)S(1)}, bf16[3,1,4,128,32]{3,4,2,1,0:T(8,128)(2,1)S(1)}, u32[]{:S(2)}, u32[]{:S(2)}) collective-permute-start(bf16[3,1,4,128,32]{3,4,2,1,0:T(8,128)(2,1)S(1)} %pad_maximum_fusion), channel_id=1, source_target_pairs={{0,1},{1,2},{2,3},{3,4},{4,5},{5,6},{6,7},{8,9},{9,10},{10,11},{11... | collective-permute-start | bytes 294920 | tf_op jit(solution)/shard_map/ppermute | solution.py:17
  22.3 0.6 collective-permute-done.3
  22.9 3.2 %collective-permute-done.2 = bf16[3,1,4,128,32]{3,4,2,1,0:T(8,128)(2,1)S(1)} collective-permute-done((bf16[3,1,4,128,32]{3,4,2,1,0:T(8,128)(2,1)S(1)}, bf16[3,1,4,128,32]{3,4,2,1,0:T(8,128)(2,1)S(1)}, u32[]{:S(2)}, u32[]{:S(2)}) %collective-permute-start.2) | collective-permute-done | bytes 98336 | tf_op jit(solution)/shard_map/ppermute | solution.py:17
  26.2 0.0 copy-done.1
  26.2 0.3 convolution_bitcast_fusion.3
  26.4 68.6 %all-gather = f32[32,64,32]{1,2,0:T(8,128)S(1)} all-gather(f32[1,64,32]{1,2,0:T(8,128)S(1)} %convolution_bitcast_fusion.3), channel_id=1, replica_groups=mesh['row'=4,'col'=8] {'row','col'}, dimensions={0}, use_global_device_ids=true | all-gather | bytes 270336 | tf_op jit(solution)/shard_map/all_gather | solution.py:51
  95.0 0.4 copy.46
  95.4 11.5 %scatter_custom_fusion = f32[256,32]{1,0:T(8,128)S(1)} fusion(s32[2048]{0:T(1024)S(1)} %compare_select_fusion, f32[2048,32]{1,0:T(8,128)S(1)} %bitcast.68, f32[]{:T(128)} %constant.48.clone.1), kind=kCustom, calls=%fused_computation.18 | custom fusion | flops 65536 | bytes 32772 | tf_op jit(solution)/shard_map/scatter-add | solution.py:47
  106.9 0.0 copy-done.2
  106.9 1.3 convolution_bitcast_fusion.1
  108.1 0.0 all-reduce.2.cloned.1.call-update
  108.2 68.8 %all-reduce.2.cloned.1.call-done = f32[512,32]{0,1:T(8,128)} async-done(((f32[512,32]{0,1:T(8,128)}), f32[512,32]{0,1:T(8,128)}) %all-reduce.2.cloned.1.call-update) | async-done | bytes 65552 | tf_op jit(solution)/shard_map/psum | solution.py:54
  177.0 6.0 %all_gather.7 = f32[2048,32]{0,1:T(8,128)S(1)} all-gather(f32[512,32]{0,1:T(8,128)} %all-reduce.2.cloned.1.call-done), channel_id=1, replica_groups=mesh['row'=4,'col'=8] {'row'}, dimensions={0}, use_global_device_ids=true | all-gather | bytes 327680 | tf_op jit(solution)/shard_map/all_gather | solution.py:55
  182.9 0.3 copy.39
  183.3 0.6 gather_fusion.1
  183.9 0.4 convolution_bitcast_fusion
  184.3 2.3 %collective-permute-start.5 = (f32[1,1,4,128,32]{3,4,2,1,0:T(8,128)S(1)}, f32[1,1,4,128,32]{3,4,2,1,0:T(8,128)S(1)}, u32[]{:S(2)}, u32[]{:S(2)}) collective-permute-start(f32[1,1,4,128,32]{3,4,2,1,0:T(8,128)S(1)} %copy.40), channel_id=1, source_target_pairs={{0,8},{8,16},{16,24},{1,9},{9,17},{17,25},{2,10},{10,18},{18,26},{... | collective-permute-start | bytes 196616 | tf_op jit(solution)/shard_map/ppermute | solution.py:17
  186.6 1.3 collective-permute-start.4
  187.9 0.0 collective-permute-done.5
  187.9 0.0 copy-start.4
  187.9 2.5 %collective-permute-done.4 = f32[1,1,4,128,32]{3,4,2,1,0:T(8,128)S(1)} collective-permute-done((f32[1,1,4,128,32]{3,4,2,1,0:T(8,128)S(1)}, f32[1,1,4,128,32]{3,4,2,1,0:T(8,128)S(1)}, u32[]{:S(2)}, u32[]{:S(2)}) %collective-permute-start.4) | collective-permute-done | bytes 65568 | tf_op jit(solution)/shard_map/ppermute | solution.py:19
  190.5 1.3 collective-permute-start.6
  191.8 4.6 %collective-permute-start.7 = (f32[3,1,4,128,32]{3,4,2,1,0:T(8,128)S(1)}, f32[3,1,4,128,32]{3,4,2,1,0:T(8,128)S(1)}, u32[]{:S(2)}, u32[]{:S(2)}) collective-permute-start(f32[3,1,4,128,32]{3,4,2,1,0:T(8,128)S(1)} %constant_dynamic-update-slice_fusion.1), channel_id=1, source_target_pairs={{0,1},{1,2},{2,3},{3,4},{4,5},{5,6},{6,7},{8,9},{9,10},{10,11},{11... | collective-permute-start | bytes 589832 | tf_op jit(solution)/shard_map/ppermute | solution.py:17
  196.4 0.0 copy-done.5
  196.4 0.0 copy-done.4
  196.4 1.8 collective-permute-done.6
  198.2 6.0 %collective-permute-done.7 = f32[3,1,4,128,32]{3,4,2,1,0:T(8,128)S(1)} collective-permute-done((f32[3,1,4,128,32]{3,4,2,1,0:T(8,128)S(1)}, f32[3,1,4,128,32]{3,4,2,1,0:T(8,128)S(1)}, u32[]{:S(2)}, u32[]{:S(2)}) %collective-permute-start.7) | collective-permute-done | bytes 196640 | tf_op jit(solution)/shard_map/ppermute | solution.py:17
  204.2 0.2 fusion.2
  204.4 0.0 copy-done
  204.4 1.1 fusion.1
  (26 shorter events, 0.1 us)
Async XLA Ops:
  6.5 197.9 %copy-start = (bf16[512,1024]{1,0:T(8,128)(2,1)S(1)}, bf16[512,1024]{1,0:T(8,128)(2,1)}, u32[]{:S(2)}) copy-start(bf16[512,1024]{1,0:T(8,128)(2,1)} %param.8) | copy-start | bytes 3145732
  6.5 0.8 copy-start.7
  6.5 170.4 %all-reduce.2.cloned.1.call-start = ((), (), s32[]{:S(2)}) async-start(), calls=%async_computation | async-start | bytes 131072 | tf_op jit(solution)/shard_map/psum | solution.py:54
  8.1 4.4 %copy-start.3 = (bf16[512,32]{0,1:T(8,128)(2,1)S(1)}, bf16[512,32]{0,1:T(8,128)(2,1)}, u32[]{:S(2)}) copy-start(bf16[512,32]{0,1:T(8,128)(2,1)} %param.6) | copy-start | bytes 98308
  8.1 4.4 %copy-start.6 = (s32[2048]{0:T(1024)S(1)}, s32[2048]{0:T(1024)}, u32[]{:S(2)}) copy-start(s32[2048]{0:T(1024)} %param.10) | copy-start | bytes 24580
  8.7 17.5 %copy-start.1 = (f32[1024,64]{0,1:T(8,128)S(1)}, f32[1024,64]{0,1:T(8,128)}, u32[]{:S(2)}) copy-start(f32[1024,64]{0,1:T(8,128)} %param.9) | copy-start | bytes 786436
  8.8 3.8 %collective-permute-start = (bf16[1,1,4,128,32]{3,4,2,1,0:T(8,128)(2,1)S(1)}, bf16[1,1,4,128,32]{3,4,2,1,0:T(8,128)(2,1)S(1)}, u32[]{:S(2)}, u32[]{:S(2)}) collective-permute-start(bf16[1,1,4,128,32]{3,4,2,1,0:T(8,128)(2,1)S(1)} %bitcast_select_fusion), channel_id=1, source_target_pairs={{0,8},{8,16},{16,24},{1,9},{9,17},{17,25},{2,10},{10,18},{18,26},{... | collective-permute-start | bytes 98312 | tf_op jit(solution)/shard_map/ppermute | solution.py:17
  11.2 5.2 %collective-permute-start.1 = (bf16[1,1,4,128,32]{3,4,2,1,0:T(8,128)(2,1)S(1)}, bf16[1,1,4,128,32]{3,4,2,1,0:T(8,128)(2,1)S(1)}, u32[]{:S(2)}, u32[]{:S(2)}) collective-permute-start(bf16[1,1,4,128,32]{3,4,2,1,0:T(8,128)(2,1)S(1)} %bitcast_select_fusion), channel_id=1, source_target_pairs={{8,0},{16,8},{24,16},{9,1},{17,9},{25,17},{10,2},{18,10},{26,18},{... | collective-permute-start | bytes 98312 | tf_op jit(solution)/shard_map/ppermute | solution.py:19
  16.4 6.5 %collective-permute-start.3 = (bf16[3,1,4,128,32]{3,4,2,1,0:T(8,128)(2,1)S(1)}, bf16[3,1,4,128,32]{3,4,2,1,0:T(8,128)(2,1)S(1)}, u32[]{:S(2)}, u32[]{:S(2)}) collective-permute-start(bf16[3,1,4,128,32]{3,4,2,1,0:T(8,128)(2,1)S(1)} %pad_maximum_fusion), channel_id=1, source_target_pairs={{1,0},{2,1},{3,2},{4,3},{5,4},{6,5},{7,6},{9,8},{10,9},{11,10},{12... | collective-permute-start | bytes 294920 | tf_op jit(solution)/shard_map/ppermute | solution.py:19
  17.7 8.4 %collective-permute-start.2 = (bf16[3,1,4,128,32]{3,4,2,1,0:T(8,128)(2,1)S(1)}, bf16[3,1,4,128,32]{3,4,2,1,0:T(8,128)(2,1)S(1)}, u32[]{:S(2)}, u32[]{:S(2)}) collective-permute-start(bf16[3,1,4,128,32]{3,4,2,1,0:T(8,128)(2,1)S(1)} %pad_maximum_fusion), channel_id=1, source_target_pairs={{0,1},{1,2},{2,3},{3,4},{4,5},{5,6},{6,7},{8,9},{9,10},{10,11},{11... | collective-permute-start | bytes 294920 | tf_op jit(solution)/shard_map/ppermute | solution.py:17
  95.0 11.9 %copy-start.2 = (f32[512,256]{1,0:T(8,128)S(1)}, f32[512,256]{1,0:T(8,128)}, u32[]{:S(2)}) copy-start(f32[512,256]{1,0:T(8,128)} %param.11) | copy-start | bytes 1572868
  184.3 3.6 %collective-permute-start.5 = (f32[1,1,4,128,32]{3,4,2,1,0:T(8,128)S(1)}, f32[1,1,4,128,32]{3,4,2,1,0:T(8,128)S(1)}, u32[]{:S(2)}, u32[]{:S(2)}) collective-permute-start(f32[1,1,4,128,32]{3,4,2,1,0:T(8,128)S(1)} %copy.40), channel_id=1, source_target_pairs={{0,8},{8,16},{16,24},{1,9},{9,17},{17,25},{2,10},{10,18},{18,26},{... | collective-permute-start | bytes 196616 | tf_op jit(solution)/shard_map/ppermute | solution.py:17
  186.6 3.9 %collective-permute-start.4 = (f32[1,1,4,128,32]{3,4,2,1,0:T(8,128)S(1)}, f32[1,1,4,128,32]{3,4,2,1,0:T(8,128)S(1)}, u32[]{:S(2)}, u32[]{:S(2)}) collective-permute-start(f32[1,1,4,128,32]{3,4,2,1,0:T(8,128)S(1)} %copy.40), channel_id=1, source_target_pairs={{8,0},{16,8},{24,16},{9,1},{17,9},{25,17},{10,2},{18,10},{26,18},{... | collective-permute-start | bytes 196616 | tf_op jit(solution)/shard_map/ppermute | solution.py:19
  187.9 8.5 %copy-start.4 = (f32[1,1,4,128,32]{3,4,2,1,0:T(8,128)}, f32[1,1,4,128,32]{3,4,2,1,0:T(8,128)S(1)}, u32[]{:S(2)}) copy-start(f32[1,1,4,128,32]{3,4,2,1,0:T(8,128)S(1)} %collective-permute-done.5) | copy-start | bytes 196612
  190.5 5.9 %copy-start.5 = (f32[1,1,4,128,32]{3,4,2,1,0:T(8,128)}, f32[1,1,4,128,32]{3,4,2,1,0:T(8,128)S(1)}, u32[]{:S(2)}) copy-start(f32[1,1,4,128,32]{3,4,2,1,0:T(8,128)S(1)} %collective-permute-done.4) | copy-start | bytes 196612
  190.5 7.7 %collective-permute-start.6 = (f32[3,1,4,128,32]{3,4,2,1,0:T(8,128)S(1)}, f32[3,1,4,128,32]{3,4,2,1,0:T(8,128)S(1)}, u32[]{:S(2)}, u32[]{:S(2)}) collective-permute-start(f32[3,1,4,128,32]{3,4,2,1,0:T(8,128)S(1)} %constant_dynamic-update-slice_fusion.1), channel_id=1, source_target_pairs={{1,0},{2,1},{3,2},{4,3},{5,4},{6,5},{7,6},{9,8},{10,9},{11,10},{12... | collective-permute-start | bytes 589832 | tf_op jit(solution)/shard_map/ppermute | solution.py:19
  191.8 12.4 %collective-permute-start.7 = (f32[3,1,4,128,32]{3,4,2,1,0:T(8,128)S(1)}, f32[3,1,4,128,32]{3,4,2,1,0:T(8,128)S(1)}, u32[]{:S(2)}, u32[]{:S(2)}) collective-permute-start(f32[3,1,4,128,32]{3,4,2,1,0:T(8,128)S(1)} %constant_dynamic-update-slice_fusion.1), channel_id=1, source_target_pairs={{0,1},{1,2},{2,3},{3,4},{4,5},{5,6},{6,7},{8,9},{9,10},{10,11},{11... | collective-permute-start | bytes 589832 | tf_op jit(solution)/shard_map/ppermute | solution.py:17
  198.2 6.0 %slice-start = ((f32[1,1,4,128,32]{3,4,2,1,0:T(8,128)}), f32[1,1,1,128,32]{3,4,2,1,0:T(8,128)S(1)}, s32[]{:S(2)}) async-start(f32[1,1,4,128,32]{3,4,2,1,0:T(8,128)} %copy-done.4), calls=%async_computation.1 | async-start | bytes 32768 | tf_op jit(solution)/shard_map/slice | solution.py:64
  198.2 6.0 %slice-start.1 = ((f32[1,1,4,128,32]{3,4,2,1,0:T(8,128)}), f32[1,1,1,128,32]{3,4,2,1,0:T(8,128)S(1)}, s32[]{:S(2)}) async-start(f32[1,1,4,128,32]{3,4,2,1,0:T(8,128)} %copy-done.5), calls=%async_computation.2 | async-start | bytes 32768 | tf_op jit(solution)/shard_map/slice | solution.py:64
Sparse Core Ops, SparseCore 0:
  108.3 68.6 all-reduce.1
where the time goes:
time: 213 us; the launch traced here: 212 us
  waiting for transfers between devices  86.8 us (41%)
  blocking collectives  74.5 us (35%)
  starting transfers between devices  18.9 us (9%)
  between operations  13.7 us (6%)
  other arithmetic  12.5 us (6%)
  matrix products  3.19 us (1%)
  local copies, waits for them, and re-layouts  2.73 us (1%)
    psum x1, waiting for transfers between devices, shards(): row_total = lax.psum(product, 'col')  68.8 us
    all_gather x1, blocking collectives, shards(): lax.all_gather(a, ('row', 'col'), axis=0, tiled=True)  68.6 us
    ppermute x4, starting transfers between devices, extended(): lax.ppermute(tail, axis, [(i, (i + 1) % count) for i in range(ends)])  13.8 us
    scatter-add x1, other arithmetic, add_piece(): return carry.at[target].add(piece, mode='drop')  11.5 us
    ppermute x4, waiting for transfers between devices, extended(): lax.ppermute(tail, axis, [(i, (i + 1) % count) for i in range(ends)])  9.19 us
    ppermute x4, waiting for transfers between devices, extended(): lax.ppermute(head, axis, [((i + 1) % count, i) for i in range(ends)])  8.76 us
    all_gather x1, blocking collectives, shards(): whole_coarse = lax.all_gather(row_total, 'row', axis=0, tiled=True)  5.97 us
    ppermute x4, starting transfers between devices, extended(): lax.ppermute(head, axis, [((i + 1) % count, i) for i in range(ends)])  5.17 us
  transfers between devices with their start and end apart: 9, of which 7 were waited for; matrix products, arithmetic and copies ran while one was open for 0% of the time, Pallas kernels for 0%

commit v1 on v0

--- a/solution.py
+++ b/solution.py
@@ -51,7 +51,11 @@
         jax.tree.map(lambda a: lax.all_gather(a, ("row", "col"), axis=0, tiled=True), partial_sums),
     )
     product = jnp.dot(coarse_inverse, column_part, precision=lax.Precision.HIGHEST)
-    row_total = lax.psum(product, "col")
+    row_total = product
+    for hop in (1, 2, 4):
+        row_total = row_total + lax.ppermute(
+            row_total, "col", [(dev, dev ^ hop) for dev in range(8)]
+        )
     whole_coarse = lax.all_gather(row_total, "row", axis=0, tiled=True)
     my_slots = lax.dynamic_slice_in_dim(
         coarse_slots, lax.axis_index(("row", "col")) * nev_count, nev_count, 0

time: 213 us -> 144 us (0.68)
  waiting for transfers between devices: 86.8 us -> 29.9 us
  between operations: 13.7 us -> 0.36 us
    psum x1 -> x0, waiting for transfers between devices: 68.8 us -> none  [shards(): row_total = lax.psum(product, 'col')]
    ppermute x0 -> x3, waiting for transfers between devices: none -> 13.7 us  [shards(): lax.ppermute(row_total, 'col', [(dev, dev ^ hop) for dev in range(8)])]
  transfers between devices with their start and end apart: 9 -> 11, of which waited for: 7 -> 9; matrix products, arithmetic and copies ran while one was open for 0% -> 0% of each run, Pallas kernels for 0% -> 0%
where the time goes in v1:
time: 144 us
  blocking collectives  76.4 us (53%)
  waiting for transfers between devices  29.9 us (21%)
  starting transfers between devices  19.1 us (13%)
  other arithmetic  12.5 us (9%)
  local copies, waits for them, and re-layouts  2.73 us (2%)
  matrix products  2.55 us (2%)
    all_gather x1, blocking collectives, shards(): lax.all_gather(a, ('row', 'col'), axis=0, tiled=True)  68.6 us
    ppermute x4, starting transfers between devices, extended(): lax.ppermute(tail, axis, [(i, (i + 1) % count) for i in range(ends)])  13.8 us
    ppermute x3, waiting for transfers between devices, shards(): lax.ppermute(row_total, 'col', [(dev, dev ^ hop) for dev in range(8)])  13.7 us
    scatter-add x1, other arithmetic, add_piece(): return carry.at[target].add(piece, mode='drop')  11.5 us
    ppermute x4, waiting for transfers between devices, extended(): lax.ppermute(head, axis, [((i + 1) % count, i) for i in range(ends)])  8.9 us
    all_gather x1, blocking collectives, shards(): whole_coarse = lax.all_gather(row_total, 'row', axis=0, tiled=True)  7.88 us
    ppermute x4, waiting for transfers between devices, extended(): lax.ppermute(tail, axis, [(i, (i + 1) % count) for i in range(ends)])  7.33 us
    ppermute x4, starting transfers between devices, extended(): lax.ppermute(head, axis, [((i + 1) % count, i) for i in range(ends)])  5.17 us
  transfers between devices with their start and end apart: 11, of which 9 were waited for; matrix products, arithmetic and copies ran while one was open for 0% of the time, Pallas kernels for 0%

profile of v1, /device:TPU:0, one launch (start us, length us, event | category | flops | bytes accessed | tf_op | source)
XLA Modules:
  0.0 143.6 jit_solution(4675946628942659227)
XLA Ops:
  0.0 0.0 copy-start
  0.0 0.8 fusion.18
  0.8 0.0 copy-done.7
  0.8 0.8 copy_bitcast_fusion
  1.6 0.0 copy-start.6
  1.6 0.0 copy-start.3
  1.6 0.6 gather_fusion
  2.1 0.0 copy-start.1
  2.2 0.1 bitcast_select_fusion
  2.2 2.4 %collective-permute-start = (bf16[1,1,4,128,32]{3,4,2,1,0:T(8,128)(2,1)S(1)}, bf16[1,1,4,128,32]{3,4,2,1,0:T(8,128)(2,1)S(1)}, u32[]{:S(2)}, u32[]{:S(2)}) collective-permute-start(bf16[1,1,4,128,32]{3,4,2,1,0:T(8,128)(2,1)S(1)} %bitcast_select_fusion), channel_id=1, source_target_pairs={{0,8},{8,16},{16,24},{1,9},{9,17},{17,25},{2,10},{10,18},{18,26},{... | collective-permute-start | bytes 98312 | tf_op jit(solution)/shard_map/ppermute | solution.py:17
  4.6 1.3 collective-permute-start.1
  5.9 0.0 copy-done.6
  6.0 0.0 copy-done.3
  6.0 0.0 collective-permute-done
  6.0 3.9 %collective-permute-done.1 = bf16[1,1,4,128,32]{3,4,2,1,0:T(8,128)(2,1)S(1)} collective-permute-done((bf16[1,1,4,128,32]{3,4,2,1,0:T(8,128)(2,1)S(1)}, bf16[1,1,4,128,32]{3,4,2,1,0:T(8,128)(2,1)S(1)}, u32[]{:S(2)}, u32[]{:S(2)}) %collective-permute-start.1) | collective-permute-done | bytes 32800 | tf_op jit(solution)/shard_map/ppermute | solution.py:19
  9.9 1.3 collective-permute-start.3
  11.2 4.6 %collective-permute-start.2 = (bf16[3,1,4,128,32]{3,4,2,1,0:T(8,128)(2,1)S(1)}, bf16[3,1,4,128,32]{3,4,2,1,0:T(8,128)(2,1)S(1)}, u32[]{:S(2)}, u32[]{:S(2)}) collective-permute-start(bf16[3,1,4,128,32]{3,4,2,1,0:T(8,128)(2,1)S(1)} %pad_maximum_fusion), channel_id=1, source_target_pairs={{0,1},{1,2},{2,3},{3,4},{4,5},{5,6},{6,7},{8,9},{9,10},{10,11},{11... | collective-permute-start | bytes 294920 | tf_op jit(solution)/shard_map/ppermute | solution.py:17
  15.7 0.6 collective-permute-done.3
  16.4 3.2 %collective-permute-done.2 = bf16[3,1,4,128,32]{3,4,2,1,0:T(8,128)(2,1)S(1)} collective-permute-done((bf16[3,1,4,128,32]{3,4,2,1,0:T(8,128)(2,1)S(1)}, bf16[3,1,4,128,32]{3,4,2,1,0:T(8,128)(2,1)S(1)}, u32[]{:S(2)}, u32[]{:S(2)}) %collective-permute-start.2) | collective-permute-done | bytes 98336 | tf_op jit(solution)/shard_map/ppermute | solution.py:17
  19.6 0.0 copy-done.1
  19.6 0.3 convolution_bitcast_fusion.3
  19.9 68.6 %all-gather = f32[32,64,32]{1,2,0:T(8,128)S(1)} all-gather(f32[1,64,32]{1,2,0:T(8,128)S(1)} %convolution_bitcast_fusion.3), channel_id=1, replica_groups=mesh['row'=4,'col'=8] {'row','col'}, dimensions={0}, use_global_device_ids=true | all-gather | bytes 270336 | tf_op jit(solution)/shard_map/all_gather | solution.py:51
  88.5 0.4 copy.48
  88.8 11.5 %scatter_custom_fusion = f32[256,32]{1,0:T(8,128)S(1)} fusion(s32[2048]{0:T(1024)S(1)} %compare_select_fusion, f32[2048,32]{1,0:T(8,128)S(1)} %bitcast.68, f32[]{:T(128)} %constant.48.clone.1), kind=kCustom, calls=%fused_computation.18 | custom fusion | flops 65536 | bytes 32772 | tf_op jit(solution)/shard_map/scatter-add | solution.py:47
  100.3 0.6 convolution_bitcast_fusion.1
  101.0 0.1 collective-permute-start.4
  101.0 4.2 %collective-permute-done.4 = f32[512,32]{0,1:T(8,128)S(1)} collective-permute-done((f32[512,32]{0,1:T(8,128)S(1)}, f32[512,32]{0,1:T(8,128)S(1)}, u32[]{:S(2)}, u32[]{:S(2)}) %collective-permute-start.4) | collective-permute-done | bytes 65568 | tf_op jit(solution)/shard_map/ppermute | solution.py:56
  105.3 0.1 collective-permute-start.5
  105.4 0.1 compare_and_fusion
  105.5 4.2 %collective-permute-done.5 = f32[512,32]{0,1:T(8,128)S(1)} collective-permute-done((f32[512,32]{0,1:T(8,128)S(1)}, f32[512,32]{0,1:T(8,128)S(1)}, u32[]{:S(2)}, u32[]{:S(2)}) %collective-permute-start.5) | collective-permute-done | bytes 65568 | tf_op jit(solution)/shard_map/ppermute | solution.py:56
  109.6 0.1 collective-permute-start.6
  109.7 5.3 %collective-permute-done.6 = f32[512,32]{0,1:T(8,128)S(1)} collective-permute-done((f32[512,32]{0,1:T(8,128)S(1)}, f32[512,32]{0,1:T(8,128)S(1)}, u32[]{:S(2)}, u32[]{:S(2)}) %collective-permute-start.6) | collective-permute-done | bytes 65568 | tf_op jit(solution)/shard_map/ppermute | solution.py:56
  115.0 7.9 %all_gather.7 = f32[2048,32]{0,1:T(8,128)S(1)} all-gather(f32[512,32]{0,1:T(8,128)S(1)} %add.58), channel_id=1, replica_groups=mesh['row'=4,'col'=8] {'row'}, dimensions={0}, use_global_device_ids=true | all-gather | bytes 327680 | tf_op jit(solution)/shard_map/all_gather | solution.py:59
  122.9 0.3 copy.41
  123.2 0.6 gather_fusion.1
  123.8 0.4 convolution_bitcast_fusion
  124.3 2.3 %collective-permute-start.8 = (f32[1,1,4,128,32]{3,4,2,1,0:T(8,128)S(1)}, f32[1,1,4,128,32]{3,4,2,1,0:T(8,128)S(1)}, u32[]{:S(2)}, u32[]{:S(2)}) collective-permute-start(f32[1,1,4,128,32]{3,4,2,1,0:T(8,128)S(1)} %copy.42), channel_id=1, source_target_pairs={{0,8},{8,16},{16,24},{1,9},{9,17},{17,25},{2,10},{10,18},{18,26},{... | collective-permute-start | bytes 196616 | tf_op jit(solution)/shard_map/ppermute | solution.py:17
  126.6 1.3 collective-permute-start.7
  127.9 0.0 collective-permute-done.8
  127.9 0.0 copy-start.4
  127.9 2.6 %collective-permute-done.7 = f32[1,1,4,128,32]{3,4,2,1,0:T(8,128)S(1)} collective-permute-done((f32[1,1,4,128,32]{3,4,2,1,0:T(8,128)S(1)}, f32[1,1,4,128,32]{3,4,2,1,0:T(8,128)S(1)}, u32[]{:S(2)}, u32[]{:S(2)}) %collective-permute-start.7) | collective-permute-done | bytes 65568 | tf_op jit(solution)/shard_map/ppermute | solution.py:19
  130.5 1.3 collective-permute-start.9
  131.8 4.6 %collective-permute-start.10 = (f32[3,1,4,128,32]{3,4,2,1,0:T(8,128)S(1)}, f32[3,1,4,128,32]{3,4,2,1,0:T(8,128)S(1)}, u32[]{:S(2)}, u32[]{:S(2)}) collective-permute-start(f32[3,1,4,128,32]{3,4,2,1,0:T(8,128)S(1)} %constant_dynamic-update-slice_fusion.1), channel_id=1, source_target_pairs={{0,1},{1,2},{2,3},{3,4},{4,5},{5,6},{6,7},{8,9},{9,10},{10,11},{11... | collective-permute-start | bytes 589832 | tf_op jit(solution)/shard_map/ppermute | solution.py:17
  136.4 1.8 %collective-permute-done.9 = f32[3,1,4,128,32]{3,4,2,1,0:T(8,128)S(1)} collective-permute-done((f32[3,1,4,128,32]{3,4,2,1,0:T(8,128)S(1)}, f32[3,1,4,128,32]{3,4,2,1,0:T(8,128)S(1)}, u32[]{:S(2)}, u32[]{:S(2)}) %collective-permute-start.9) | collective-permute-done | bytes 196640 | tf_op jit(solution)/shard_map/ppermute | solution.py:19
  138.2 4.1 %collective-permute-done.10 = f32[3,1,4,128,32]{3,4,2,1,0:T(8,128)S(1)} collective-permute-done((f32[3,1,4,128,32]{3,4,2,1,0:T(8,128)S(1)}, f32[3,1,4,128,32]{3,4,2,1,0:T(8,128)S(1)}, u32[]{:S(2)}, u32[]{:S(2)}) %collective-permute-start.10) | collective-permute-done | bytes 196640 | tf_op jit(solution)/shard_map/ppermute | solution.py:17
  142.3 0.0 slice-done
  142.3 0.2 fusion.2
  142.6 1.1 fusion.1
  (32 shorter events, 0.2 us)
Async XLA Ops:
  0.0 142.6 %copy-start = (bf16[512,1024]{1,0:T(8,128)(2,1)S(1)}, bf16[512,1024]{1,0:T(8,128)(2,1)}, u32[]{:S(2)}) copy-start(bf16[512,1024]{1,0:T(8,128)(2,1)} %param.8) | copy-start | bytes 3145732
  0.0 0.8 copy-start.7
  1.6 4.4 %copy-start.6 = (s32[2048]{0:T(1024)S(1)}, s32[2048]{0:T(1024)}, u32[]{:S(2)}) copy-start(s32[2048]{0:T(1024)} %param.10) | copy-start | bytes 24580
  1.6 4.4 %copy-start.3 = (bf16[512,32]{0,1:T(8,128)(2,1)S(1)}, bf16[512,32]{0,1:T(8,128)(2,1)}, u32[]{:S(2)}) copy-start(bf16[512,32]{0,1:T(8,128)(2,1)} %param.6) | copy-start | bytes 98308
  2.1 17.5 %copy-start.1 = (f32[1024,64]{0,1:T(8,128)S(1)}, f32[1024,64]{0,1:T(8,128)}, u32[]{:S(2)}) copy-start(f32[1024,64]{0,1:T(8,128)} %param.9) | copy-start | bytes 786436
  2.2 3.8 %collective-permute-start = (bf16[1,1,4,128,32]{3,4,2,1,0:T(8,128)(2,1)S(1)}, bf16[1,1,4,128,32]{3,4,2,1,0:T(8,128)(2,1)S(1)}, u32[]{:S(2)}, u32[]{:S(2)}) collective-permute-start(bf16[1,1,4,128,32]{3,4,2,1,0:T(8,128)(2,1)S(1)} %bitcast_select_fusion), channel_id=1, source_target_pairs={{0,8},{8,16},{16,24},{1,9},{9,17},{17,25},{2,10},{10,18},{18,26},{... | collective-permute-start | bytes 98312 | tf_op jit(solution)/shard_map/ppermute | solution.py:17
  4.6 5.2 %collective-permute-start.1 = (bf16[1,1,4,128,32]{3,4,2,1,0:T(8,128)(2,1)S(1)}, bf16[1,1,4,128,32]{3,4,2,1,0:T(8,128)(2,1)S(1)}, u32[]{:S(2)}, u32[]{:S(2)}) collective-permute-start(bf16[1,1,4,128,32]{3,4,2,1,0:T(8,128)(2,1)S(1)} %bitcast_select_fusion), channel_id=1, source_target_pairs={{8,0},{16,8},{24,16},{9,1},{17,9},{25,17},{10,2},{18,10},{26,18},{... | collective-permute-start | bytes 98312 | tf_op jit(solution)/shard_map/ppermute | solution.py:19
  9.9 6.5 %collective-permute-start.3 = (bf16[3,1,4,128,32]{3,4,2,1,0:T(8,128)(2,1)S(1)}, bf16[3,1,4,128,32]{3,4,2,1,0:T(8,128)(2,1)S(1)}, u32[]{:S(2)}, u32[]{:S(2)}) collective-permute-start(bf16[3,1,4,128,32]{3,4,2,1,0:T(8,128)(2,1)S(1)} %pad_maximum_fusion), channel_id=1, source_target_pairs={{1,0},{2,1},{3,2},{4,3},{5,4},{6,5},{7,6},{9,8},{10,9},{11,10},{12... | collective-permute-start | bytes 294920 | tf_op jit(solution)/shard_map/ppermute | solution.py:19
  11.2 8.4 %collective-permute-start.2 = (bf16[3,1,4,128,32]{3,4,2,1,0:T(8,128)(2,1)S(1)}, bf16[3,1,4,128,32]{3,4,2,1,0:T(8,128)(2,1)S(1)}, u32[]{:S(2)}, u32[]{:S(2)}) collective-permute-start(bf16[3,1,4,128,32]{3,4,2,1,0:T(8,128)(2,1)S(1)} %pad_maximum_fusion), channel_id=1, source_target_pairs={{0,1},{1,2},{2,3},{3,4},{4,5},{5,6},{6,7},{8,9},{9,10},{10,11},{11... | collective-permute-start | bytes 294920 | tf_op jit(solution)/shard_map/ppermute | solution.py:17
  88.5 11.9 %copy-start.2 = (f32[512,256]{1,0:T(8,128)S(1)}, f32[512,256]{1,0:T(8,128)}, u32[]{:S(2)}) copy-start(f32[512,256]{1,0:T(8,128)} %param.11) | copy-start | bytes 1572868
  101.0 4.3 %collective-permute-start.4 = (f32[512,32]{0,1:T(8,128)S(1)}, f32[512,32]{0,1:T(8,128)S(1)}, u32[]{:S(2)}, u32[]{:S(2)}) collective-permute-start(f32[512,32]{0,1:T(8,128)S(1)} %convolution_bitcast_fusion.1), channel_id=1, source_target_pairs={{0,1},{1,0},{2,3},{3,2},{4,5},{5,4},{6,7},{7,6},{8,9},{9,8},{10,11... | collective-permute-start | bytes 196616 | tf_op jit(solution)/shard_map/ppermute | solution.py:56
  105.3 4.3 %collective-permute-start.5 = (f32[512,32]{0,1:T(8,128)S(1)}, f32[512,32]{0,1:T(8,128)S(1)}, u32[]{:S(2)}, u32[]{:S(2)}) collective-permute-start(f32[512,32]{0,1:T(8,128)S(1)} %add.56), channel_id=1, source_target_pairs={{0,2},{1,3},{2,0},{3,1},{4,6},{5,7},{6,4},{7,5},{8,10},{9,11},{10,... | collective-permute-start | bytes 196616 | tf_op jit(solution)/shard_map/ppermute | solution.py:56
  109.6 5.4 %collective-permute-start.6 = (f32[512,32]{0,1:T(8,128)S(1)}, f32[512,32]{0,1:T(8,128)S(1)}, u32[]{:S(2)}, u32[]{:S(2)}) collective-permute-start(f32[512,32]{0,1:T(8,128)S(1)} %add.57), channel_id=1, source_target_pairs={{0,4},{1,5},{2,6},{3,7},{4,0},{5,1},{6,2},{7,3},{8,12},{9,13},{10,... | collective-permute-start | bytes 196616 | tf_op jit(solution)/shard_map/ppermute | solution.py:56
  124.3 3.6 %collective-permute-start.8 = (f32[1,1,4,128,32]{3,4,2,1,0:T(8,128)S(1)}, f32[1,1,4,128,32]{3,4,2,1,0:T(8,128)S(1)}, u32[]{:S(2)}, u32[]{:S(2)}) collective-permute-start(f32[1,1,4,128,32]{3,4,2,1,0:T(8,128)S(1)} %copy.42), channel_id=1, source_target_pairs={{0,8},{8,16},{16,24},{1,9},{9,17},{17,25},{2,10},{10,18},{18,26},{... | collective-permute-start | bytes 196616 | tf_op jit(solution)/shard_map/ppermute | solution.py:17
  126.6 3.9 %collective-permute-start.7 = (f32[1,1,4,128,32]{3,4,2,1,0:T(8,128)S(1)}, f32[1,1,4,128,32]{3,4,2,1,0:T(8,128)S(1)}, u32[]{:S(2)}, u32[]{:S(2)}) collective-permute-start(f32[1,1,4,128,32]{3,4,2,1,0:T(8,128)S(1)} %copy.42), channel_id=1, source_target_pairs={{8,0},{16,8},{24,16},{9,1},{17,9},{25,17},{10,2},{18,10},{26,18},{... | collective-permute-start | bytes 196616 | tf_op jit(solution)/shard_map/ppermute | solution.py:19
  127.9 8.5 %copy-start.4 = (f32[1,1,4,128,32]{3,4,2,1,0:T(8,128)}, f32[1,1,4,128,32]{3,4,2,1,0:T(8,128)S(1)}, u32[]{:S(2)}) copy-start(f32[1,1,4,128,32]{3,4,2,1,0:T(8,128)S(1)} %collective-permute-done.8) | copy-start | bytes 196612
  130.5 5.9 %copy-start.5 = (f32[1,1,4,128,32]{3,4,2,1,0:T(8,128)}, f32[1,1,4,128,32]{3,4,2,1,0:T(8,128)S(1)}, u32[]{:S(2)}) copy-start(f32[1,1,4,128,32]{3,4,2,1,0:T(8,128)S(1)} %collective-permute-done.7) | copy-start | bytes 196612
  130.5 7.7 %collective-permute-start.9 = (f32[3,1,4,128,32]{3,4,2,1,0:T(8,128)S(1)}, f32[3,1,4,128,32]{3,4,2,1,0:T(8,128)S(1)}, u32[]{:S(2)}, u32[]{:S(2)}) collective-permute-start(f32[3,1,4,128,32]{3,4,2,1,0:T(8,128)S(1)} %constant_dynamic-update-slice_fusion.1), channel_id=1, source_target_pairs={{1,0},{2,1},{3,2},{4,3},{5,4},{6,5},{7,6},{9,8},{10,9},{11,10},{12... | collective-permute-start | bytes 589832 | tf_op jit(solution)/shard_map/ppermute | solution.py:19
  131.8 10.5 %collective-permute-start.10 = (f32[3,1,4,128,32]{3,4,2,1,0:T(8,128)S(1)}, f32[3,1,4,128,32]{3,4,2,1,0:T(8,128)S(1)}, u32[]{:S(2)}, u32[]{:S(2)}) collective-permute-start(f32[3,1,4,128,32]{3,4,2,1,0:T(8,128)S(1)} %constant_dynamic-update-slice_fusion.1), channel_id=1, source_target_pairs={{0,1},{1,2},{2,3},{3,4},{4,5},{5,6},{6,7},{8,9},{9,10},{10,11},{11... | collective-permute-start | bytes 589832 | tf_op jit(solution)/shard_map/ppermute | solution.py:17
  138.2 4.1 %slice-start = ((f32[1,1,4,128,32]{3,4,2,1,0:T(8,128)}), f32[1,1,1,128,32]{3,4,2,1,0:T(8,128)S(1)}, s32[]{:S(2)}) async-start(f32[1,1,4,128,32]{3,4,2,1,0:T(8,128)} %copy-done.4), calls=%async_computation | async-start | bytes 32768 | tf_op jit(solution)/shard_map/slice | solution.py:68
  138.2 4.1 %slice-start.1 = ((f32[1,1,4,128,32]{3,4,2,1,0:T(8,128)}), f32[1,1,1,128,32]{3,4,2,1,0:T(8,128)S(1)}, s32[]{:S(2)}) async-start(f32[1,1,4,128,32]{3,4,2,1,0:T(8,128)} %copy-done.5), calls=%async_computation.1 | async-start | bytes 32768 | tf_op jit(solution)/shard_map/slice | solution.py:68
